TPU v7x, 32 devices: a whole 2x2x4 slice. The times are simulated.
32 devices in a mesh: gx: 4 (over y, x), gy: 2 (over core), gz: 4 (over z).
Axes of the slice: x: 2, y: 2, z: 4, core: 2. Of those that a mesh axis runs over, the one named last changes fastest.
Arguments:
- measures: float32 [65536, 256], P(('gx', 'gy', 'gz')), may hold values from -6 to 6
- group_index: int32 [65536], P(('gx', 'gy', 'gz')), may hold values from 0 to 511, as said below
- distinct_keys: int32 [32, 512], P(('gx', 'gy', 'gz')), may hold values from 32 to 65567, as said below
- group_counts: int32 [32], P(('gx', 'gy', 'gz')), may hold values from 128 to 512, as said below
Outputs:
- group_sums: float32 [16384, 256], P(('gx', 'gy', 'gz'))
- group_rows: int32 [16384], P(('gx', 'gy', 'gz'))
- group_keys: int32 [16384], P(('gx', 'gy', 'gz'))
- group_total: int32 [], replicated
Inputs may be any that keep to these rules, and one draw needn't show every extreme that they name: `group_counts`: every device has between 128 and 512 groups, and some device has exactly 512. `group_index`: each row's index lies below its device's group count, and every group of a device has at least one row. `distinct_keys`: each device's keys rise strictly; all keys of device d equal d modulo 32, so no key lives on two devices; entries at and past the device's count are unused.
All inputs are finite; a program needn't handle non-finite values.
Results may differ from a plain program's by a relative error of at most 0.0003.
Values sent between devices are 32-bit elements; how exact they have to be, the bound alone decides.
No kernel may reach another device: no remote copies, remote signals or barrier semaphores. Data moves between devices by JAX's collectives and lax.ppermute only.
A program may use at most 64 MiB of HBM per device.

v0:
```python
import jax
import jax.numpy as jnp
from jax import lax
from jax.sharding import PartitionSpec as P


def shards(measures, group_index, distinct_keys, group_counts):
    rows, width = measures.shape
    span = distinct_keys.shape[1]
    devices = lax.axis_size(("gx", "gy", "gz"))
    slots = span // devices
    plane = lax.axis_size("gx") * lax.axis_size("gy")
    line = lax.axis_size("gz")
    count = group_counts[0]
    myself = jnp.int32(0)
    sender_counts = lax.all_gather(group_counts, ("gx", "gy", "gz"), axis=0, tiled=True)
    sender_offsets = jnp.cumsum(sender_counts) - sender_counts
    myself = lax.axis_index(("gx", "gy", "gz"))
    offset = sender_offsets[myself]
    group_total = jnp.sum(sender_counts)
    block = min(1024, rows)
    labels = lax.broadcasted_iota(jnp.int32, (span, block), 0)

    def accumulate(step, carry):
        totals, tallies = carry
        start = step * block
        index = lax.dynamic_slice_in_dim(group_index, start, block)
        values = lax.dynamic_slice_in_dim(measures, start, block, 0)
        hits = index[None, :] == labels
        totals = totals + jnp.dot(
            hits.astype(jnp.float32),
            values,
            precision=lax.Precision.HIGHEST,
            preferred_element_type=jnp.float32,
        )
        tallies = tallies + jnp.sum(hits, axis=1, dtype=jnp.int32)
        return (totals, tallies)

    sums, tallies = lax.fori_loop(
        0,
        rows // block,
        accumulate,
        (jnp.zeros((span, width), jnp.float32), jnp.zeros((span,), jnp.int32)),
    )
    local = jnp.arange(span, dtype=jnp.int32)
    live = local < count
    keys = jnp.where(live, distinct_keys[0], -1)
    fields = jnp.stack([tallies.astype(jnp.float32), keys.astype(jnp.float32)], axis=1)
    extra = fields.shape[1]

    def arrange(array):
        shaped = array.reshape((slots, devices) + array.shape[1:])
        rolled = jnp.roll(shaped, offset, axis=1)
        return rolled.reshape((slots, plane, line) + array.shape[1:])

    outgoing = (arrange(sums), arrange(fields))
    arrived = (
        lax.all_to_all(
            lax.all_to_all(outgoing[0], "gz", split_axis=2, concat_axis=2, tiled=True),
            ("gx", "gy"),
            split_axis=1,
            concat_axis=1,
            tiled=True,
        ),
        lax.all_to_all(
            lax.all_to_all(outgoing[1], "gz", split_axis=2, concat_axis=2, tiled=True),
            ("gx", "gy"),
            split_axis=1,
            concat_axis=1,
            tiled=True,
        ),
    )
    got_sums, got_fields = arrived
    got_fields = got_fields.reshape(-1, extra)
    sender = jnp.arange(devices, dtype=jnp.int32).reshape(1, plane, line)
    start_of = sender_offsets.reshape(1, plane, line)
    count_of = sender_counts.reshape(1, plane, line)
    level = jnp.arange(slots, dtype=jnp.int32).reshape(slots, 1, 1)
    position = level * devices + (myself - start_of) % devices
    arrived_live = (position < count_of) & (sender >= 0)
    target = jnp.where(arrived_live, (start_of + position) // devices, span).reshape(-1)
    group_sums = (
        jnp.zeros((span, width), jnp.float32)
        .at[target]
        .set(got_sums.reshape(-1, width), mode="drop")
    )
    group_rows = (
        jnp.zeros((span,), jnp.int32)
        .at[target]
        .set(got_fields[:, 0].astype(jnp.int32), mode="drop")
    )
    group_keys = (
        jnp.full((span,), -1, jnp.int32)
        .at[target]
        .set(got_fields[:, 1].astype(jnp.int32), mode="drop")
    )
    return (group_sums, group_rows, group_keys, group_total)


def solution(mesh):
    return jax.shard_map(
        shards,
        mesh=mesh,
        in_specs=(
            P(("gx", "gy", "gz"), None),
            P(("gx", "gy", "gz")),
            P(("gx", "gy", "gz"), None),
            P(("gx", "gy", "gz")),
        ),
        out_specs=(P(("gx", "gy", "gz"), None), P(("gx", "gy", "gz")), P(("gx", "gy", "gz")), P()),
        check_vma=False,
    )
```

profile of v0, /device:TPU:0, one launch (start us, length us, event | category | flops | bytes accessed | tf_op | source)
XLA Modules:
  0.0 106.3 jit_solution(15189355763401430567)
XLA Ops:
  1.4 42.0 %all-reduce = s32[32]{0:T(128)S(1)} all-reduce(s32[32]{0:T(128)S(1)} %dynamic-update-slice), channel_id=1, replica_groups=mesh['gx'=4,'gy'=2,'gz'=4] {'gx','gy','gz'}, use_global_device_ids=true, to_apply=%add | all-reduce | flops 32 | bytes 256
  46.8 7.4 %while.16 = (s32[]{:T(128)}, f32[512,256]{1,0:T(8,128)S(1)}, s32[512]{0:T(512)S(1)}, s32[2048]{0:T(1024)}, f32[2048,256]{1,0:T(8,128)}, /*index=5*/s32[]{:T(128)}, s32[]{:T(128)}, s32[]{:T(128)}, s32[]{:T(128)}) while((s32[]{:T(128)}, f32[512,256]{1,0:T(8,128)S(1)}, s32[512]{0:T(512)S(1)}, s32[2048]{0:T(1024)}, ...), condition=%wide.region_3.4_spmd.clone, body=%wide.region_1.3_spmd.clone.sunk | while | flops 1612972544 | bytes 2121886 | solution.py:39
  46.9 0.7 dynamic_slice.55
  47.6 2.7 %fusion.24 = f32[512,256]{1,0:T(8,128)S(1)} fusion(f32[2048,256]{1,0:T(8,128)} %get-tuple-element.203, s32[]{:T(128)S(6)} %select_n.107, s32[1024]{0:T(1024)S(1)} %dynamic_slice.55, f32[512,256]{1,0:T(8,128)S(1)} %get-tuple-element.191, pred[]{:T(512)S(6)} %compare.20), kind=kOutput, calls=%fused_computation.8.clone.1 | convolution fusion | flops 1611399168 | bytes 2101253 | tf_op jit(solution)/shard_map/while/body/eval_jaxpr/dot_general | solution.py:30
  50.6 0.7 dynamic_slice.55
  51.2 2.7 %fusion.24 = f32[512,256]{1,0:T(8,128)S(1)} fusion(f32[2048,256]{1,0:T(8,128)} %get-tuple-element.203, s32[]{:T(128)S(6)} %select_n.107, s32[1024]{0:T(1024)S(1)} %dynamic_slice.55, f32[512,256]{1,0:T(8,128)S(1)} %get-tuple-element.191, pred[]{:T(512)S(6)} %compare.20), kind=kOutput, calls=%fused_computation.8.clone.1 | convolution fusion | flops 1611399168 | bytes 2101253 | tf_op jit(solution)/shard_map/while/body/eval_jaxpr/dot_general | solution.py:30
  54.8 0.7 reduce.5
  55.8 0.7 reshape.312
  56.5 3.6 %all-to-all-start.2 = ((f32[4,1,256]{2,1,0:T(1,128)}), f32[4,1,256]{2,1,0:T(1,128)S(1)}, u32[]{:S(2)}, u32[]{:S(2)}) async-start(f32[4,1,256]{2,1,0:T(1,128)} %reshape.312), calls=%async_computation.2 | async-start | bytes 8192 | tf_op jit(solution)/shard_map/all_to_all | solution.py:66
  60.5 1.1 %copy.39 = f32[16,8,4,256]{3,1,0,2:T(8,128)} copy(f32[16,8,4,256]{3,0,2,1:T(8,128)S(1)} %bitcast.23) | data formatting | bytes 1048576 | tf_op jit(solution)/shard_map/reshape | solution.py:54
  61.6 4.0 %all-to-all-done.2 = f32[4,1,256]{2,1,0:T(1,128)S(1)} async-done(((f32[4,1,256]{2,1,0:T(1,128)}), f32[4,1,256]{2,1,0:T(1,128)S(1)}, u32[]{:S(2)}, u32[]{:S(2)}) %all-to-all-start.2) | async-done | bytes 4128 | tf_op jit(solution)/shard_map/all_to_all | solution.py:66
  65.6 3.5 %all-to-all-start = ((f32[16,8,4,256]{3,1,0,2:T(8,128)}), f32[16,8,4,256]{3,1,0,2:T(8,128)S(1)}, u32[]{:S(2)}, u32[]{:S(2)}) async-start(f32[16,8,4,256]{3,1,0,2:T(8,128)} %copy.39), calls=%async_computation | async-start | bytes 1048576 | tf_op jit(solution)/shard_map/all_to_all | solution.py:59
  69.8 0.7 reduce.6
  70.6 0.7 reshape.314
  71.3 10.3 %all-to-all-done = f32[16,8,4,256]{3,1,0,2:T(8,128)S(1)} async-done(((f32[16,8,4,256]{3,1,0,2:T(8,128)}), f32[16,8,4,256]{3,1,0,2:T(8,128)S(1)}, u32[]{:S(2)}, u32[]{:S(2)}) %all-to-all-start) | async-done | bytes 524320 | tf_op jit(solution)/shard_map/all_to_all | solution.py:59
  81.6 3.6 %all-to-all-start.3 = ((f32[8,1,128]{2,1,0:T(1,128)}), f32[8,1,128]{2,1,0:T(1,128)S(1)}, u32[]{:S(2)}, u32[]{:S(2)}) async-start(f32[8,1,128]{2,1,0:T(1,128)} %reshape.314), calls=%async_computation.3 | async-start | bytes 8192 | tf_op jit(solution)/shard_map/all_to_all | solution.py:65
  85.2 1.1 %copy.40 = f32[16,8,4,256]{3,2,0,1:T(4,128)} copy(f32[16,8,4,256]{3,1,0,2:T(8,128)S(1)} %all-to-all-done) | data formatting | bytes 1048576 | tf_op jit(solution)/shard_map/all_to_all | solution.py:59
  86.4 3.5 %all-to-all-done.3 = f32[8,1,128]{2,1,0:T(1,128)S(1)} async-done(((f32[8,1,128]{2,1,0:T(1,128)}), f32[8,1,128]{2,1,0:T(1,128)S(1)}, u32[]{:S(2)}, u32[]{:S(2)}) %all-to-all-start.3) | async-done | bytes 4128 | tf_op jit(solution)/shard_map/all_to_all | solution.py:65
  89.8 3.5 %all-to-all-start.1 = ((f32[16,8,4,256]{3,2,0,1:T(4,128)}), f32[16,8,4,256]{3,2,0,1:T(4,128)S(1)}, u32[]{:S(2)}, u32[]{:S(2)}) async-start(f32[16,8,4,256]{3,2,0,1:T(4,128)} %copy.40), calls=%async_computation.1 | async-start | bytes 1048576 | tf_op jit(solution)/shard_map/all_to_all | solution.py:58
  93.7 0.7 reduce.7
  94.8 3.0 %scatter_custom_fusion.1 = s32[512]{0:T(512)} fusion(s32[512]{0:T(512)S(1)} %bitcast.30, s32[512]{0:T(512)S(1)} %bitcast.34, s32[]{:T(128)} %constant.107.clone.1), kind=kCustom, calls=%fused_computation.40 | custom fusion | bytes 2052 | tf_op jit(solution)/shard_map/scatter | solution.py:90
  97.8 3.0 %scatter_custom_fusion.2 = s32[512]{0:T(512)} fusion(s32[512]{0:T(512)S(1)} %bitcast.31, s32[512]{0:T(512)S(1)} %bitcast.33, s32[]{:T(128)} %constant.111.clone.1), kind=kCustom, calls=%fused_computation.38 | custom fusion | bytes 2052 | tf_op jit(solution)/shard_map/scatter | solution.py:95
  100.8 2.2 %all-to-all-done.1 = f32[16,8,4,256]{3,2,0,1:T(4,128)S(1)} async-done(((f32[16,8,4,256]{3,2,0,1:T(4,128)}), f32[16,8,4,256]{3,2,0,1:T(4,128)S(1)}, u32[]{:S(2)}, u32[]{:S(2)}) %all-to-all-start.1) | async-done | bytes 524320 | tf_op jit(solution)/shard_map/all_to_all | solution.py:58
  103.2 3.0 %scatter_custom_fusion = f32[512,256]{1,0:T(8,128)} fusion(s32[512]{0:T(512)S(1)} %bitcast.32, f32[512,256]{1,0:T(8,128)S(1)} %reshape.271, f32[]{:T(128)} %constant.100.clone.1), kind=kCustom, calls=%fused_computation.16 | custom fusion | bytes 524292 | tf_op jit(solution)/shard_map/scatter | solution.py:85
  (44 shorter events, 5.3 us)
Async XLA Ops:
  46.8 8.0 %copy-start = (s32[1,512]{1,0:T(1,128)S(1)}, s32[1,512]{1,0:T(1,128)}, u32[]{:S(2)}) copy-start(s32[1,512]{1,0:T(1,128)} %param.8) | copy-start | bytes 6148
  56.5 9.2 %all-to-all-start.2 = ((f32[4,1,256]{2,1,0:T(1,128)}), f32[4,1,256]{2,1,0:T(1,128)S(1)}, u32[]{:S(2)}, u32[]{:S(2)}) async-start(f32[4,1,256]{2,1,0:T(1,128)} %reshape.312), calls=%async_computation.2 | async-start | bytes 8192 | tf_op jit(solution)/shard_map/all_to_all | solution.py:66
  65.6 16.0 %all-to-all-start = ((f32[16,8,4,256]{3,1,0,2:T(8,128)}), f32[16,8,4,256]{3,1,0,2:T(8,128)S(1)}, u32[]{:S(2)}, u32[]{:S(2)}) async-start(f32[16,8,4,256]{3,1,0,2:T(8,128)} %copy.39), calls=%async_computation | async-start | bytes 1048576 | tf_op jit(solution)/shard_map/all_to_all | solution.py:59
  81.6 8.2 %all-to-all-start.3 = ((f32[8,1,128]{2,1,0:T(1,128)}), f32[8,1,128]{2,1,0:T(1,128)S(1)}, u32[]{:S(2)}, u32[]{:S(2)}) async-start(f32[8,1,128]{2,1,0:T(1,128)} %reshape.314), calls=%async_computation.3 | async-start | bytes 8192 | tf_op jit(solution)/shard_map/all_to_all | solution.py:65
  89.8 13.2 %all-to-all-start.1 = ((f32[16,8,4,256]{3,2,0,1:T(4,128)}), f32[16,8,4,256]{3,2,0,1:T(4,128)S(1)}, u32[]{:S(2)}, u32[]{:S(2)}) async-start(f32[16,8,4,256]{3,2,0,1:T(4,128)} %copy.40), calls=%async_computation.1 | async-start | bytes 1048576 | tf_op jit(solution)/shard_map/all_to_all | solution.py:58
where the time goes:
time: 107 us; the launch traced here: 106 us
  blocking collectives  42 us (39%)
  waiting for transfers between devices  20.1 us (19%)
  local copies, waits for them, and re-layouts  17.5 us (16%)
  starting transfers between devices  14.1 us (13%)
  matrix products  5.34 us (5%)
  other arithmetic  3.86 us (4%)
  between operations  3.41 us (3%)
    unnamed x1, blocking collectives  42 us
    all_to_all x1, waiting for transfers between devices, shards(): lax.all_to_all(outgoing[0], 'gz', split_axis=2, concat_axis=2, tiled=True)  10.3 us
    dot_general x2, matrix products, accumulate(): jnp.dot(hits.astype(jnp.float32), values, precision=lax.Precision.HIGHEST...  5.34 us
    all_to_all x1, waiting for transfers between devices, shards(): lax.all_to_all(outgoing[1], 'gz', split_axis=2, concat_axis=2, tiled=True)  4.02 us
    all_to_all x1, starting transfers between devices, shards(): lax.all_to_all(outgoing[1], 'gz', split_axis=2, concat_axis=2, tiled=True)  3.6 us
    all_to_all x1, starting transfers between devices, shards(): lax.all_to_all(lax.all_to_all(outgoing[1], 'gz', split_axis=2, concat_axi...  3.56 us
    all_to_all x1, starting transfers between devices, shards(): lax.all_to_all(lax.all_to_all(outgoing[0], 'gz', split_axis=2, concat_axi...  3.49 us
    all_to_all x1, starting transfers between devices, shards(): lax.all_to_all(outgoing[0], 'gz', split_axis=2, concat_axis=2, tiled=True)  3.47 us
  transfers between devices with their start and end apart: 4, of which 4 were waited for; matrix products, arithmetic and copies ran while one was open for 12% of the time, Pallas kernels for 0%

commit v1 on v0

v1 whole, which is shorter than its diff:
```python
import functools

import jax
import jax.numpy as jnp
from jax import lax
from jax.experimental import pallas as pl
from jax.experimental.pallas import tpu as pltpu
from jax.sharding import PartitionSpec as P

AXES = ("gx", "gy", "gz")
LANES = 128


def split3(x):
    high = x.astype(jnp.bfloat16)
    rest = x - high.astype(jnp.float32)
    middle = rest.astype(jnp.bfloat16)
    low = (rest - middle.astype(jnp.float32)).astype(jnp.bfloat16)
    return high, middle, low


def local_kernel(devices, slots, index_ref, values_ref, keys_ref, packed_ref, sums_ref, fields_ref):
    step = pl.program_id(0)
    span, width = sums_ref.shape
    rows = values_ref.shape[0]
    parts = width // LANES
    each = slots * parts + 1

    @pl.when(step == 0)
    def _():
        sums_ref[...] = jnp.zeros_like(sums_ref)
        fields_ref[...] = keys_ref[...]

    index = index_ref[...]
    residue = index % devices
    level = index // devices
    place = residue * slots + level
    hits = (place == lax.broadcasted_iota(jnp.int32, (span, rows), 0)).astype(jnp.bfloat16)
    total = sums_ref[...]
    for part in split3(values_ref[...]):
        total = total + jnp.dot(hits, part, preferred_element_type=jnp.float32)
    sums_ref[...] = total
    by_residue = (residue == lax.broadcasted_iota(jnp.int32, (devices, rows), 0)).astype(jnp.bfloat16)
    by_level = (level == lax.broadcasted_iota(jnp.int32, (LANES, rows), 0)).astype(jnp.bfloat16)
    fields_ref[...] += lax.dot_general(
        by_residue, by_level, (((1,), (1,)), ((), ())), preferred_element_type=jnp.float32
    )

    @pl.when(step == pl.num_programs(0) - 1)
    def _():
        for device in range(devices):
            for copy in (device, device + devices):
                start = copy * each
                for part in range(parts):
                    packed_ref[start + part * slots : start + (part + 1) * slots, :] = sums_ref[
                        device * slots : (device + 1) * slots, part * LANES : (part + 1) * LANES
                    ]
                packed_ref[start + each - 1 : start + each, :] = fields_ref[device : device + 1, :]


def place_kernel(devices, slots, counts_ref, me_ref, got_ref, sums_ref, rows_ref, keys_ref, room_ref, mask_ref):
    span, width = sums_ref.shape
    parts = width // LANES
    each = slots * parts + 1
    me = me_ref[0]
    room_ref[...] = jnp.zeros_like(room_ref)
    window = room_ref.shape[0] - span
    spot = lax.broadcasted_iota(jnp.int32, (1, span), 1)
    line = lax.broadcasted_iota(jnp.int32, (window, width), 0)
    padding = jnp.zeros((window - slots, width), jnp.float32)
    offset = jnp.int32(0)
    end = jnp.int32(0)
    level = jnp.zeros((1, span), jnp.int32)
    for sender in range(devices):
        base = end
        offset = offset + counts_ref[sender]
        end = lax.div(offset - me + (devices - 1), devices)
        first = sender * each
        chunk = jnp.concatenate(
            [got_ref[first + part * slots : first + (part + 1) * slots, :] for part in range(parts)], axis=1
        )
        shift = base % 8
        chunk = pltpu.roll(jnp.concatenate([chunk, padding], axis=0), shift, 0)
        there = pl.ds(pl.multiple_of(base - shift, 8), window)
        room_ref[there, :] = jnp.where((line >= shift) & (line < shift + end - base), chunk, room_ref[there, :])
        inside = (spot >= base) & (spot < end)
        mask_ref[sender : sender + 1, :] = inside.astype(jnp.float32)
        level = jnp.where(inside, spot - base, level)
    sums_ref[...] = room_ref[:span, :]
    fields = jnp.concatenate(
        [got_ref[(sender + 1) * each - 1 : (sender + 1) * each, :] for sender in range(devices)], axis=0
    )
    picked = lax.dot_general(
        fields,
        mask_ref[...],
        (((0,), (0,)), ((), ())),
        precision=lax.Precision.HIGHEST,
        preferred_element_type=jnp.float32,
    )
    field = lax.broadcasted_iota(jnp.int32, (LANES, span), 0)
    rows = jnp.sum(jnp.where(field == level, picked, 0.0), axis=0, keepdims=True)
    keys = jnp.sum(jnp.where(field == level + slots, picked, 0.0), axis=0, keepdims=True)
    live = spot < end
    rows = jnp.where(live, rows, 0.0).astype(jnp.int32)
    keys = jnp.where(live, keys, -1.0).astype(jnp.int32)
    for part in range(span // LANES):
        rows_ref[part : part + 1, :] = rows[:, part * LANES : (part + 1) * LANES]
        keys_ref[part : part + 1, :] = keys[:, part * LANES : (part + 1) * LANES]


def shards(measures, group_index, distinct_keys, group_counts):
    rows, width = measures.shape
    span = distinct_keys.shape[1]
    devices = lax.axis_size(AXES)
    slots = span // devices
    parts = width // LANES
    each = slots * parts + 1
    me = lax.axis_index(AXES)
    counts = lax.all_to_all(
        jnp.broadcast_to(group_counts.reshape(1, 1, 1), (devices, 1, LANES)), AXES, split_axis=0, concat_axis=0, tiled=True
    )[:, 0, 0]
    keys = distinct_keys[0].reshape(slots, devices).T.astype(jnp.float32)
    keys = jnp.pad(keys, ((0, 0), (slots, LANES - 2 * slots)))
    block = min(512, rows)
    packed = pl.pallas_call(
        functools.partial(local_kernel, devices, slots),
        grid=(rows // block,),
        in_specs=[
            pl.BlockSpec((1, block), lambda i: (0, i)),
            pl.BlockSpec((block, width), lambda i: (i, 0)),
            pl.BlockSpec((devices, LANES), lambda i: (0, 0)),
        ],
        out_specs=pl.BlockSpec((2 * devices * each, LANES), lambda i: (0, 0)),
        out_shape=jax.ShapeDtypeStruct((2 * devices * each, LANES), jnp.float32),
        scratch_shapes=[pltpu.VMEM((span, width), jnp.float32), pltpu.VMEM((devices, LANES), jnp.float32)],
        cost_estimate=pl.CostEstimate(flops=6 * span * rows * width, bytes_accessed=4 * rows * width, transcendentals=0),
        name="local",
    )(group_index.reshape(1, rows), measures, keys)
    ahead = jnp.arange(devices, dtype=jnp.int32) < me
    offset = jnp.sum(jnp.where(ahead, counts, 0)) % devices
    outgoing = lax.dynamic_slice_in_dim(packed.reshape(2 * devices, 1, each * LANES), devices - offset, devices, 0)
    got = lax.all_to_all(outgoing, AXES, split_axis=0, concat_axis=0, tiled=True)
    group_total = jnp.sum(counts)
    group_sums, group_rows, group_keys = pl.pallas_call(
        functools.partial(place_kernel, devices, slots),
        in_specs=[
            pl.BlockSpec(memory_space=pltpu.SMEM),
            pl.BlockSpec(memory_space=pltpu.SMEM),
            pl.BlockSpec(memory_space=pltpu.VMEM),
        ],
        out_specs=[pl.BlockSpec(memory_space=pltpu.VMEM)] * 3,
        out_shape=[
            jax.ShapeDtypeStruct((span, width), jnp.float32),
            jax.ShapeDtypeStruct((span // LANES, LANES), jnp.int32),
            jax.ShapeDtypeStruct((span // LANES, LANES), jnp.int32),
        ],
        scratch_shapes=[pltpu.VMEM((span + -(-slots // 8) * 8 + 8, width), jnp.float32), pltpu.VMEM((devices, span), jnp.float32)],
        name="place",
    )(counts, me.reshape(1), got.reshape(devices * each, LANES))
    return group_sums, group_rows.reshape(span), group_keys.reshape(span), group_total


def solution(mesh):
    return jax.shard_map(
        shards,
        mesh=mesh,
        in_specs=(P(AXES, None), P(AXES), P(AXES, None), P(AXES)),
        out_specs=(P(AXES, None), P(AXES), P(AXES), P()),
        check_vma=False,
    )
```

time: 107 us -> 44.7 us (0.42)
  the two profiles are of different devices: /device:TPU:0 before, /device:TPU:1 now
where the time goes in v1:
time: 44.7 us; the launch traced here: 44.4 us
  blocking collectives  21.4 us (48%)
  Pallas kernels  7.57 us (17%)
  starting transfers between devices  7.08 us (16%)
  between operations  3.26 us (7%)
  local copies, waits for them, and re-layouts  2.55 us (6%)
  other arithmetic  2.54 us (6%)
    all_to_all x1, blocking collectives, shards(): lax.all_to_all(outgoing, AXES, split_axis=0, concat_axis=0, tiled=True)  21.4 us
    all_to_all x1, starting transfers between devices, shards(): lax.all_to_all(jnp.broadcast_to(group_counts.reshape(1, 1, 1), (devices,...  7.08 us
    pallas_call x1, Pallas kernels, shards(): pl.pallas_call(functools.partial(local_kernel, devices, slots), grid=(row...  5.15 us
    pallas_call x1, Pallas kernels, shards(): pl.pallas_call(functools.partial(place_kernel, devices, slots), in_specs=...  2.42 us
    reduce_sum x1, other arithmetic, shards(): group_total = jnp.sum(counts)  1.2 us
    dynamic_slice x1, local copies, waits for them, and re-layouts, shards(): lax.dynamic_slice_in_dim(packed.reshape(2 * devices, 1, each * LANES), de...  1.1 us
  transfers between devices with their start and end apart: 1, of which 0 were waited for; matrix products, arithmetic and copies ran while one was open for 3% of the time, Pallas kernels for 12%

profile of v1, /device:TPU:1, one launch (start us, length us, event | category | flops | bytes accessed | tf_op | source)
XLA Modules:
  0.0 44.4 jit_solution(10706737771469308062)
XLA Ops:
  1.3 0.6 %broadcast_in_dim.12 = s32[32,1,128]{2,1,0:T(1,128)} broadcast(s32[]{:T(128)} %bitcast.8), dimensions={} | broadcast | bytes 16388 | tf_op jit(solution)/shard_map/broadcast_in_dim | solution.py:120
  1.9 7.1 %all-to-all-start = ((s32[32,1,128]{2,1,0:T(1,128)}), s32[32,1,128]{2,1,0:T(1,128)S(1)}, u32[]{:S(2)}, u32[]{:S(2)}) async-start(s32[32,1,128]{2,1,0:T(1,128)} %broadcast_in_dim.12), calls=%async_computation | async-start | bytes 32768 | tf_op jit(solution)/shard_map/all_to_all | solution.py:119
  9.0 0.7 %convert_reduce_fusion = f32[512]{0:T(512)S(1)} fusion(s32[1,512]{1,0:T(1,128)} %param.6), kind=kLoop, calls=%fused_computation.2 | loop fusion | flops 512 | bytes 4096 | tf_op jit(solution)/shard_map/convert_element_type | solution.py:122
  9.7 0.1 convert_element_type.12
  9.8 0.1 copy.11
  9.8 0.7 %pad.4.keys_ref = f32[32,128]{1,0:T(8,128)} pad(f32[32,16]{1,0:T(8,128)S(1)} %bitcast.11, f32[]{:T(128)} %constant.30.clone.1), padding=0_0x16_96 | pad | bytes 18436 | tf_op jit(solution)/shard_map/jit(_pad)/pad | solution.py:123
  10.5 5.2 %local.1 = f32[2112,128]{1,0:T(8,128)} custom-call(s32[1,2048]{1,0:T(1,128)} %bitcast.12, f32[2048,256]{1,0:T(8,128)} %values_ref.1, f32[32,128]{1,0:T(8,128)} %pad.4.keys_ref), custom_call_target="tpu_custom_call" | custom-call | flops 1610612736 | bytes 2097152 | tf_op jit(solution)/shard_map/local/pallas_call | solution.py:125
  15.7 0.0 all-to-all-done
  15.7 1.2 %slice_reduce_fusion = (s32[]{:T(128)}, s32[32]{0:T(128)S(1)}) fusion(s32[32,1,128]{2,1,0:T(1,128)S(1)} %all-to-all-done), kind=kLoop, calls=%fused_computation | loop fusion | flops 31 | bytes 260 | tf_op jit(solution)/shard_map/reduce_sum | solution.py:143
  16.9 0.0 copy-start
  16.9 0.6 %fusion = s32[]{:T(128)} fusion(s32[32]{0:T(128)S(1)} %get-tuple-element.11.counts_ref, s32[]{:T(128)} %add.17), kind=kLoop, calls=%fused_computation.4 | loop fusion | flops 95 | bytes 136 | tf_op jit(solution)/shard_map/reduce_sum | solution.py:140
  19.5 1.1 %constant_dynamic-slice_fusion = f32[32,1,4224]{2,1,0:T(1,128)S(1)} fusion(f32[64,1,4224]{2,1,0:T(1,128)} %bitcast.10, s32[]{:T(128)S(6)} %select_n.16), kind=kLoop, calls=%fused_computation.5 | loop fusion | bytes 1081348 | tf_op jit(solution)/shard_map/dynamic_slice | solution.py:141
  20.6 21.4 %all_to_all.10 = f32[32,1,4224]{2,1,0:T(1,128)} all-to-all(f32[32,1,4224]{2,1,0:T(1,128)S(1)} %constant_dynamic-slice_fusion), channel_id=1, replica_groups=mesh['gx'=4,'gy'=2,'gz'=4] {'gx','gy','gz'}, dimensions={0} | all-to-all | bytes 1081344 | tf_op jit(solution)/shard_map/all_to_all | solution.py:142
  41.9 0.0 copy-done
  41.9 2.4 %place.1 = (f32[512,256]{1,0:T(8,128)}, s32[4,128]{1,0:T(4,128)}, s32[4,128]{1,0:T(4,128)}) custom-call(s32[32]{0:T(128)} %copy-done, s32[1]{0:T(128)} %bitcast.1.me_ref, f32[1056,128]{1,0:T(8,128)} %bitcast.9), custom_call_target="tpu_custom_call" | custom-call | tf_op jit(solution)/shard_map/place/pallas_call | solution.py:144
Async XLA Ops:
  1.9 13.8 %all-to-all-start = ((s32[32,1,128]{2,1,0:T(1,128)}), s32[32,1,128]{2,1,0:T(1,128)S(1)}, u32[]{:S(2)}, u32[]{:S(2)}) async-start(s32[32,1,128]{2,1,0:T(1,128)} %broadcast_in_dim.12), calls=%async_computation | async-start | bytes 32768 | tf_op jit(solution)/shard_map/all_to_all | solution.py:119
  16.9 25.1 %copy-start = (s32[32]{0:T(128)}, s32[32]{0:T(128)S(1)}, u32[]{:S(2)}) copy-start(s32[32]{0:T(128)S(1)} %get-tuple-element.11.counts_ref) | copy-start | bytes 388

commit v2 on v1

--- a/solution.py
+++ b/solution.py
@@ -58,22 +58,73 @@
                 packed_ref[start + each - 1 : start + each, :] = fields_ref[device : device + 1, :]
 
 
-def place_kernel(devices, slots, counts_ref, me_ref, got_ref, sums_ref, rows_ref, keys_ref, room_ref, mask_ref):
+def spread_kernel(count_ref, out_ref):
+    out_ref[...] = jnp.full(out_ref.shape, count_ref[0], jnp.int32)
+
+
+def roll_kernel(devices, pieces, me_ref, counts_ref, packed_ref, out_ref, room_ref, in_sem, out_sem):
+    counts = counts_ref[...].astype(jnp.float32)
+    sender = lax.broadcasted_iota(jnp.int32, counts.shape, 0)
+    lane = lax.broadcasted_iota(jnp.int32, counts.shape, 1)
+    offset = jnp.sum(jnp.where((sender < me_ref[0]) & (lane == 0), counts, 0.0)).astype(jnp.int32)
+    start = devices - lax.rem(offset, devices)
+    each = devices // pieces
+    into = [
+        pltpu.make_async_copy(
+            packed_ref.at[pl.ds(start + piece * each, each)], room_ref.at[pl.ds(piece * each, each)], in_sem.at[piece]
+        )
+        for piece in range(pieces)
+    ]
+    out = [
+        pltpu.make_async_copy(
+            room_ref.at[pl.ds(piece * each, each)], out_ref.at[pl.ds(piece * each, each)], out_sem.at[piece]
+        )
+        for piece in range(pieces)
+    ]
+    for copy in into:
+        copy.start()
+    for piece in range(pieces):
+        into[piece].wait()
+        out[piece].start()
+    for copy in out:
+        copy.wait()
+
+
+def place_kernel(
+    devices, slots, pieces, me_ref, held_ref, all_ref, sums_ref, rows_ref, keys_ref, total_ref,
+    counts_ref, got_ref, room_ref, mask_ref, counts_sem, sem
+):
     span, width = sums_ref.shape
     parts = width // LANES
     each = slots * parts + 1
     me = me_ref[0]
+    group = devices // pieces
+    copies = [
+        pltpu.make_async_copy(
+            all_ref.at[pl.ds(piece * group * each, group * each)],
+            got_ref.at[pl.ds(piece * group * each, group * each)],
+            sem.at[piece],
+        )
+        for piece in range(pieces)
+    ]
+    counts_copy = pltpu.make_async_copy(held_ref, counts_ref, counts_sem)
+    counts_copy.start()
+    for copy in copies:
+        copy.start()
     room_ref[...] = jnp.zeros_like(room_ref)
     window = room_ref.shape[0] - span
     spot = lax.broadcasted_iota(jnp.int32, (1, span), 1)
     line = lax.broadcasted_iota(jnp.int32, (window, width), 0)
     padding = jnp.zeros((window - slots, width), jnp.float32)
+    counts_copy.wait()
     offset = jnp.int32(0)
     end = jnp.int32(0)
     level = jnp.zeros((1, span), jnp.int32)
     for sender in range(devices):
+        if sender % group == 0:
+            copies[sender // group].wait()
         base = end
-        offset = offset + counts_ref[sender]
+        offset = offset + counts_ref[sender, 0]
         end = lax.div(offset - me + (devices - 1), devices)
         first = sender * each
         chunk = jnp.concatenate(
@@ -87,6 +138,7 @@
         mask_ref[sender : sender + 1, :] = inside.astype(jnp.float32)
         level = jnp.where(inside, spot - base, level)
     sums_ref[...] = room_ref[:span, :]
+    total_ref[0] = offset
     fields = jnp.concatenate(
         [got_ref[(sender + 1) * each - 1 : (sender + 1) * each, :] for sender in range(devices)], axis=0
     )
@@ -116,9 +168,16 @@
     parts = width // LANES
     each = slots * parts + 1
     me = lax.axis_index(AXES)
-    counts = lax.all_to_all(
-        jnp.broadcast_to(group_counts.reshape(1, 1, 1), (devices, 1, LANES)), AXES, split_axis=0, concat_axis=0, tiled=True
-    )[:, 0, 0]
+    pieces = 4
+    spread = pl.pallas_call(
+        spread_kernel,
+        in_specs=[pl.BlockSpec(memory_space=pltpu.SMEM)],
+        out_specs=pl.BlockSpec(memory_space=pltpu.VMEM),
+        out_shape=jax.ShapeDtypeStruct((devices, LANES), jnp.int32),
+        name="spread",
+    )(group_counts)
+    counts = lax.all_to_all(spread.reshape(devices, 1, LANES), AXES, split_axis=0, concat_axis=0, tiled=True)
+    counts = counts.reshape(devices, LANES)
     keys = distinct_keys[0].reshape(slots, devices).T.astype(jnp.float32)
     keys = jnp.pad(keys, ((0, 0), (slots, LANES - 2 * slots)))
     block = min(512, rows)
@@ -136,28 +195,48 @@
         cost_estimate=pl.CostEstimate(flops=6 * span * rows * width, bytes_accessed=4 * rows * width, transcendentals=0),
         name="local",
     )(group_index.reshape(1, rows), measures, keys)
-    ahead = jnp.arange(devices, dtype=jnp.int32) < me
-    offset = jnp.sum(jnp.where(ahead, counts, 0)) % devices
-    outgoing = lax.dynamic_slice_in_dim(packed.reshape(2 * devices, 1, each * LANES), devices - offset, devices, 0)
-    got = lax.all_to_all(outgoing, AXES, split_axis=0, concat_axis=0, tiled=True)
-    group_total = jnp.sum(counts)
-    group_sums, group_rows, group_keys = pl.pallas_call(
-        functools.partial(place_kernel, devices, slots),
+    outgoing = pl.pallas_call(
+        functools.partial(roll_kernel, devices, pieces),
         in_specs=[
             pl.BlockSpec(memory_space=pltpu.SMEM),
+            pl.BlockSpec(memory_space=pltpu.VMEM),
+            pl.BlockSpec(memory_space=pl.ANY),
+        ],
+        out_specs=pl.BlockSpec(memory_space=pl.ANY),
+        out_shape=jax.ShapeDtypeStruct((devices, 1, each * LANES), jnp.float32),
+        scratch_shapes=[
+            pltpu.VMEM((devices, 1, each * LANES), jnp.float32),
+            pltpu.SemaphoreType.DMA((pieces,)),
+            pltpu.SemaphoreType.DMA((pieces,)),
+        ],
+        name="roll",
+    )(me.reshape(1), counts, packed.reshape(2 * devices, 1, each * LANES))
+    got = lax.all_to_all(outgoing, AXES, split_axis=0, concat_axis=0, tiled=True)
+    group_sums, group_rows, group_keys, group_total = pl.pallas_call(
+        functools.partial(place_kernel, devices, slots, pieces),
+        in_specs=[
             pl.BlockSpec(memory_space=pltpu.SMEM),
             pl.BlockSpec(memory_space=pltpu.VMEM),
-        ],
-        out_specs=[pl.BlockSpec(memory_space=pltpu.VMEM)] * 3,
+            pl.BlockSpec(memory_space=pl.ANY),
+        ],
+        out_specs=[pl.BlockSpec(memory_space=pltpu.VMEM)] * 3 + [pl.BlockSpec(memory_space=pltpu.SMEM)],
         out_shape=[
             jax.ShapeDtypeStruct((span, width), jnp.float32),
             jax.ShapeDtypeStruct((span // LANES, LANES), jnp.int32),
             jax.ShapeDtypeStruct((span // LANES, LANES), jnp.int32),
-        ],
-        scratch_shapes=[pltpu.VMEM((span + -(-slots // 8) * 8 + 8, width), jnp.float32), pltpu.VMEM((devices, span), jnp.float32)],
+            jax.ShapeDtypeStruct((1,), jnp.int32),
+        ],
+        scratch_shapes=[
+            pltpu.SMEM((devices, LANES), jnp.int32),
+            pltpu.VMEM((devices * each, LANES), jnp.float32),
+            pltpu.VMEM((span + -(-slots // 8) * 8 + 8, width), jnp.float32),
+            pltpu.VMEM((devices, span), jnp.float32),
+            pltpu.SemaphoreType.DMA,
+            pltpu.SemaphoreType.DMA((pieces,)),
+        ],
         name="place",
-    )(counts, me.reshape(1), got.reshape(devices * each, LANES))
-    return group_sums, group_rows.reshape(span), group_keys.reshape(span), group_total
+    )(me.reshape(1), counts, got.reshape(devices * each, LANES))
+    return group_sums, group_rows.reshape(span), group_keys.reshape(span), group_total.reshape(())
 
 
 def solution(mesh):

time: 44.7 us -> 44 us (0.984)
  Pallas kernels: 7.57 us -> 11.5 us
  between operations: 3.26 us -> 1.3 us
  other arithmetic: 2.54 us -> 0.7 us
  local copies, waits for them, and re-layouts: 2.55 us -> 1.44 us
    pallas_call x1 -> x3, Pallas kernels: 2.42 us -> 6.36 us  [the longest x1 3.09 us: shards(): pl.pallas_call(functools.partial(place_kernel, devices, slots, pieces), i...]
    reduce_sum x2 -> x0, other arithmetic: 1.83 us -> none  [the longest x1 1.2 us: shards(): group_total = jnp.sum(counts)]
    dynamic_slice x1 -> x0, local copies, waits for them, and re-layouts: 1.1 us -> none  [shards(): lax.dynamic_slice_in_dim(packed.reshape(2 * devices, 1, each * LANES), de...]
    broadcast_in_dim x1 -> x0, local copies, waits for them, and re-layouts: 0.62 us -> none  [shards(): jnp.broadcast_to(group_counts.reshape(1, 1, 1), (devices, 1, LANES))]
    unnamed x2, local copies, waits for them, and re-layouts: 0.01 us -> 0.6 us
  transfers between devices with their start and end apart: 1 -> 1, of which waited for: 0 -> 0; matrix products, arithmetic and copies ran while one was open for 3% -> 4% of each run, Pallas kernels for 12% -> 12%
where the time goes in v2:
time: 44 us; the launch traced here: 43.6 us
  blocking collectives  21.6 us (49%)
  Pallas kernels  11.5 us (26%)
  starting transfers between devices  7.08 us (16%)
  local copies, waits for them, and re-layouts  1.44 us (3%)
  between operations  1.3 us (3%)
  other arithmetic  0.7 us (2%)
    all_to_all x1, blocking collectives, shards(): lax.all_to_all(outgoing, AXES, split_axis=0, concat_axis=0, tiled=True)  21.6 us
    all_to_all x1, starting transfers between devices, shards(): lax.all_to_all(spread.reshape(devices, 1, LANES), AXES, split_axis=0, con...  7.08 us
    pallas_call x1, Pallas kernels, shards(): pl.pallas_call(functools.partial(local_kernel, devices, slots), grid=(row...  5.14 us
    pallas_call x1, Pallas kernels, shards(): pl.pallas_call(functools.partial(place_kernel, devices, slots, pieces), i...  3.09 us
    pallas_call x1, Pallas kernels, shards(): pl.pallas_call(functools.partial(roll_kernel, devices, pieces), in_specs=...  2.67 us
  transfers between devices with their start and end apart: 1, of which 0 were waited for; matrix products, arithmetic and copies ran while one was open for 4% of the time, Pallas kernels for 12%

profile of v2, /device:TPU:1, one launch (start us, length us, event | category | flops | bytes accessed | tf_op | source)
XLA Modules:
  0.0 43.6 jit_solution(16351159980844608018)
XLA Ops:
  1.3 0.6 %spread.1 = s32[32,128]{1,0:T(8,128)} custom-call(s32[1]{0:T(128)S(6)} %copy.11.count_ref), custom_call_target="tpu_custom_call" | custom-call | tf_op jit(solution)/shard_map/spread/pallas_call | solution.py:172
  1.9 7.1 %all-to-all-start = ((s32[32,1,128]{2,1,0:T(1,128)}), s32[32,1,128]{2,1,0:T(1,128)S(1)}, u32[]{:S(2)}, u32[]{:S(2)}) async-start(s32[32,1,128]{2,1,0:T(1,128)} %bitcast.16), calls=%async_computation | async-start | bytes 32768 | tf_op jit(solution)/shard_map/all_to_all | solution.py:179
  9.0 0.7 %convert_reduce_fusion = f32[512]{0:T(512)S(1)} fusion(s32[1,512]{1,0:T(1,128)} %param.6), kind=kLoop, calls=%fused_computation | loop fusion | flops 512 | bytes 4096 | tf_op jit(solution)/shard_map/convert_element_type | solution.py:181
  9.7 0.1 convert_element_type.12
  9.8 0.1 copy.10
  9.8 0.7 %pad.4.keys_ref = f32[32,128]{1,0:T(8,128)} pad(f32[32,16]{1,0:T(8,128)S(1)} %bitcast.17, f32[]{:T(128)} %constant.18.clone.1), padding=0_0x16_96 | pad | bytes 18436 | tf_op jit(solution)/shard_map/jit(_pad)/pad | solution.py:182
  10.5 5.1 %local.1 = f32[2112,128]{1,0:T(8,128)} custom-call(s32[1,2048]{1,0:T(1,128)} %bitcast.18, f32[2048,256]{1,0:T(8,128)} %values_ref.1, f32[32,128]{1,0:T(8,128)} %pad.4.keys_ref), custom_call_target="tpu_custom_call" | custom-call | flops 1610612736 | bytes 2097152 | tf_op jit(solution)/shard_map/local/pallas_call | solution.py:184
  15.7 0.0 all-to-all-done
  15.7 0.0 copy-start
  15.7 0.6 %copy-done = s32[32,1,128]{2,1,0:T(1,128)} copy-done((s32[32,1,128]{2,1,0:T(1,128)}, s32[32,1,128]{2,1,0:T(1,128)S(1)}, u32[]{:S(2)}) %copy-start) | copy-done | bytes 16408
  16.3 2.7 %roll.1 = f32[32,1,4224]{2,1,0:T(1,128)} custom-call(s32[1]{0:T(128)} %bitcast.me_ref, s32[32,128]{1,0:T(8,128)} %bitcast.14, f32[64,1,4224]{2,1,0:T(1,128)} %bitcast.13), custom_call_target="tpu_custom_call" | custom-call | tf_op jit(solution)/shard_map/roll/pallas_call | solution.py:198
  18.9 21.6 %all_to_all.10 = f32[32,1,4224]{2,1,0:T(1,128)} all-to-all(f32[32,1,4224]{2,1,0:T(1,128)} %roll.1), channel_id=1, replica_groups=mesh['gx'=4,'gy'=2,'gz'=4] {'gx','gy','gz'}, dimensions={0} | all-to-all | bytes 1081344 | tf_op jit(solution)/shard_map/all_to_all | solution.py:214
  40.5 3.1 %place.1 = (f32[512,256]{1,0:T(8,128)}, s32[4,128]{1,0:T(4,128)}, s32[4,128]{1,0:T(4,128)}, s32[1]{0:T(128)}) custom-call(s32[1]{0:T(128)} %bitcast.me_ref, s32[32,128]{1,0:T(8,128)} %bitcast.15, f32[1056,128]{1,0:T(8,128)} %bitcast.12), custom_call_target="tpu_custom_call" | custom-call | tf_op jit(solution)/shard_map/place/pallas_call | solution.py:215
Async XLA Ops:
  1.9 13.8 %all-to-all-start = ((s32[32,1,128]{2,1,0:T(1,128)}), s32[32,1,128]{2,1,0:T(1,128)S(1)}, u32[]{:S(2)}, u32[]{:S(2)}) async-start(s32[32,1,128]{2,1,0:T(1,128)} %bitcast.16), calls=%async_computation | async-start | bytes 32768 | tf_op jit(solution)/shard_map/all_to_all | solution.py:179
  15.7 0.6 %copy-start = (s32[32,1,128]{2,1,0:T(1,128)}, s32[32,1,128]{2,1,0:T(1,128)S(1)}, u32[]{:S(2)}) copy-start(s32[32,1,128]{2,1,0:T(1,128)S(1)} %all-to-all-done) | copy-start | bytes 49156

commit v3 on v2

v3 whole, which is shorter than its diff:
```python
import functools

import jax
import jax.numpy as jnp
from jax import lax
from jax.experimental import pallas as pl
from jax.experimental.pallas import tpu as pltpu
from jax.sharding import PartitionSpec as P

AXES = ("gx", "gy", "gz")
LANES = 128
MIB = 1024 * 1024


def split3(x):
    high = x.astype(jnp.bfloat16)
    rest = x - high.astype(jnp.float32)
    middle = rest.astype(jnp.bfloat16)
    low = (rest - middle.astype(jnp.float32)).astype(jnp.bfloat16)
    return high, middle, low


def local_kernel(devices, slots, block, index_ref, values_ref, keys_ref, packed_ref, sums_ref, fields_ref):
    span, width = sums_ref.shape
    rows = values_ref.shape[0]
    parts = width // LANES
    each = slots * parts + 1

    def one_hot(height, place):
        return place == lax.broadcasted_iota(jnp.int32, (height, place.shape[1]), 0)

    def across(left, right):
        return lax.dot_general(left, right, (((1,), (1,)), ((), ())), preferred_element_type=jnp.float32)

    group = lax.broadcasted_iota(jnp.int32, (1, span), 1)
    to_residue = one_hot(devices, group % devices).astype(jnp.bfloat16)
    to_level = jnp.where(one_hot(LANES, group // devices + slots), keys_ref[...].astype(jnp.float32), 0.0)
    fields = jnp.zeros(fields_ref.shape, jnp.float32)
    for part in split3(to_level):
        fields = fields + across(to_residue, part)
    for start in range(0, rows, block):
        index = index_ref[:, start : start + block]
        residue = index % devices
        level = index // devices
        hits = one_hot(span, residue * slots + level).astype(jnp.bfloat16)
        high, middle, low = split3(values_ref[start : start + block, :])
        total = jnp.dot(hits, high, preferred_element_type=jnp.float32)
        total = total + jnp.dot(hits, middle, preferred_element_type=jnp.float32)
        total = total + jnp.dot(hits, low, preferred_element_type=jnp.float32)
        sums_ref[...] = total if start == 0 else sums_ref[...] + total
        fields = fields + across(
            one_hot(devices, residue).astype(jnp.bfloat16), one_hot(LANES, level).astype(jnp.bfloat16)
        )
    fields_ref[...] = fields
    for device in range(devices):
        for copy in (device, device + devices):
            start = copy * each
            for part in range(parts):
                packed_ref[start + part * slots : start + (part + 1) * slots, :] = sums_ref[
                    device * slots : (device + 1) * slots, part * LANES : (part + 1) * LANES
                ]
            packed_ref[start + each - 1 : start + each, :] = fields_ref[device : device + 1, :]


def spread_kernel(count_ref, out_ref):
    out_ref[...] = jnp.full(out_ref.shape, count_ref[0], jnp.int32)


def roll_kernel(devices, me_ref, counts_ref, packed_ref, out_ref, sem):
    counts = counts_ref[...].astype(jnp.float32)
    sender = lax.broadcasted_iota(jnp.int32, counts.shape, 0)
    lane = lax.broadcasted_iota(jnp.int32, counts.shape, 1)
    offset = jnp.sum(jnp.where((sender < me_ref[0]) & (lane == 0), counts, 0.0)).astype(jnp.int32)
    start = devices - lax.rem(offset, devices)
    copy = pltpu.make_async_copy(packed_ref.at[pl.ds(start, devices)], out_ref, sem)
    copy.start()
    copy.wait()


def place_kernel(
    devices, slots, me_ref, held_ref, got_ref, sums_ref, rows_ref, keys_ref, total_ref,
    counts_ref, room_ref, mask_ref, counts_sem
):
    span, width = sums_ref.shape
    parts = width // LANES
    each = slots * parts + 1
    me = me_ref[0]
    counts_copy = pltpu.make_async_copy(held_ref, counts_ref, counts_sem)
    counts_copy.start()
    room_ref[...] = jnp.zeros_like(room_ref)
    window = room_ref.shape[0] - span
    spot = lax.broadcasted_iota(jnp.int32, (1, span), 1)
    line = lax.broadcasted_iota(jnp.int32, (window, width), 0)
    padding = jnp.zeros((window - slots, width), jnp.float32)
    counts_copy.wait()
    offset = jnp.int32(0)
    end = jnp.int32(0)
    level = jnp.zeros((1, span), jnp.int32)
    for sender in range(devices):
        base = end
        offset = offset + counts_ref[sender, 0]
        end = lax.div(offset - me + (devices - 1), devices)
        first = sender * each
        chunk = jnp.concatenate(
            [got_ref[first + part * slots : first + (part + 1) * slots, :] for part in range(parts)], axis=1
        )
        shift = base % 8
        chunk = pltpu.roll(jnp.concatenate([chunk, padding], axis=0), shift, 0)
        there = pl.ds(pl.multiple_of(base - shift, 8), window)
        room_ref[there, :] = jnp.where((line >= shift) & (line < shift + end - base), chunk, room_ref[there, :])
        inside = (spot >= base) & (spot < end)
        mask_ref[sender : sender + 1, :] = inside.astype(jnp.float32)
        level = jnp.where(inside, spot - base, level)
    sums_ref[...] = room_ref[:span, :]
    total_ref[0] = offset
    fields = jnp.concatenate(
        [got_ref[(sender + 1) * each - 1 : (sender + 1) * each, :] for sender in range(devices)], axis=0
    )
    picked = lax.dot_general(
        fields,
        mask_ref[...],
        (((0,), (0,)), ((), ())),
        precision=lax.Precision.HIGHEST,
        preferred_element_type=jnp.float32,
    )
    field = lax.broadcasted_iota(jnp.int32, (LANES, span), 0)
    rows = jnp.sum(jnp.where(field == level, picked, 0.0), axis=0, keepdims=True)
    keys = jnp.sum(jnp.where(field == level + slots, picked, 0.0), axis=0, keepdims=True)
    live = spot < end
    rows = jnp.where(live, rows, 0.0).astype(jnp.int32)
    keys = jnp.where(live, keys, -1.0).astype(jnp.int32)
    for part in range(span // LANES):
        rows_ref[part : part + 1, :] = rows[:, part * LANES : (part + 1) * LANES]
        keys_ref[part : part + 1, :] = keys[:, part * LANES : (part + 1) * LANES]


def shards(measures, group_index, distinct_keys, group_counts):
    rows, width = measures.shape
    span = distinct_keys.shape[1]
    devices = lax.axis_size(AXES)
    slots = span // devices
    parts = width // LANES
    each = slots * parts + 1
    me = lax.axis_index(AXES)
    spread = pl.pallas_call(
        spread_kernel,
        in_specs=[pl.BlockSpec(memory_space=pltpu.SMEM)],
        out_specs=pl.BlockSpec(memory_space=pltpu.VMEM),
        out_shape=jax.ShapeDtypeStruct((devices, LANES), jnp.int32),
        compiler_params=pltpu.CompilerParams(vmem_limit_bytes=MIB),
        name="spread",
    )(group_counts)
    counts = lax.all_to_all(spread.reshape(devices, 1, LANES), AXES, split_axis=0, concat_axis=0, tiled=True)
    counts = counts.reshape(devices, LANES)
    packed = pl.pallas_call(
        functools.partial(local_kernel, devices, slots, min(512, rows)),
        in_specs=[pl.BlockSpec(memory_space=pltpu.VMEM)] * 3,
        out_specs=pl.BlockSpec(memory_space=pltpu.VMEM),
        out_shape=jax.ShapeDtypeStruct((2 * devices * each, LANES), jnp.float32),
        scratch_shapes=[pltpu.VMEM((span, width), jnp.float32), pltpu.VMEM((devices, LANES), jnp.float32)],
        cost_estimate=pl.CostEstimate(flops=6 * span * rows * width, bytes_accessed=4 * rows * width, transcendentals=0),
        compiler_params=pltpu.CompilerParams(vmem_limit_bytes=16 * MIB),
        name="local",
    )(group_index.reshape(1, rows), measures, distinct_keys)
    outgoing = pl.pallas_call(
        functools.partial(roll_kernel, devices),
        in_specs=[
            pl.BlockSpec(memory_space=pltpu.SMEM),
            pl.BlockSpec(memory_space=pltpu.VMEM),
            pl.BlockSpec(memory_space=pltpu.VMEM),
        ],
        out_specs=pl.BlockSpec(memory_space=pltpu.HBM),
        out_shape=jax.ShapeDtypeStruct((devices, 1, each * LANES), jnp.float32),
        scratch_shapes=[pltpu.SemaphoreType.DMA],
        compiler_params=pltpu.CompilerParams(vmem_limit_bytes=4 * MIB),
        name="roll",
    )(me.reshape(1), counts, packed.reshape(2 * devices, 1, each * LANES))
    got = lax.all_to_all(outgoing, AXES, split_axis=0, concat_axis=0, tiled=True)
    group_sums, group_rows, group_keys, group_total = pl.pallas_call(
        functools.partial(place_kernel, devices, slots),
        in_specs=[
            pl.BlockSpec(memory_space=pltpu.SMEM),
            pl.BlockSpec(memory_space=pltpu.VMEM),
            pl.BlockSpec(memory_space=pltpu.VMEM),
        ],
        out_specs=[pl.BlockSpec(memory_space=pltpu.VMEM)] * 3 + [pl.BlockSpec(memory_space=pltpu.SMEM)],
        out_shape=[
            jax.ShapeDtypeStruct((span, width), jnp.float32),
            jax.ShapeDtypeStruct((span // LANES, LANES), jnp.int32),
            jax.ShapeDtypeStruct((span // LANES, LANES), jnp.int32),
            jax.ShapeDtypeStruct((1,), jnp.int32),
        ],
        scratch_shapes=[
            pltpu.SMEM((devices, LANES), jnp.int32),
            pltpu.VMEM((span + -(-slots // 8) * 8 + 8, width), jnp.float32),
            pltpu.VMEM((devices, span), jnp.float32),
            pltpu.SemaphoreType.DMA,
        ],
        compiler_params=pltpu.CompilerParams(vmem_limit_bytes=8 * MIB),
        name="place",
    )(me.reshape(1), counts, got.reshape(devices * each, LANES))
    return group_sums, group_rows.reshape(span), group_keys.reshape(span), group_total.reshape(())


def solution(mesh):
    return jax.shard_map(
        shards,
        mesh=mesh,
        in_specs=(P(AXES, None), P(AXES), P(AXES, None), P(AXES)),
        out_specs=(P(AXES, None), P(AXES), P(AXES), P()),
        check_vma=False,
    )
```

time: 44 us -> 38 us (0.86)
  Pallas kernels: 11.5 us -> 5.06 us
  blocking collectives: 21.6 us -> 19.7 us
  waiting for transfers between devices: 0.01 us -> 1.54 us
  local copies, waits for them, and re-layouts: 1.44 us -> 2.96 us
  other arithmetic: 0.7 us -> 0 us
    pallas_call x3, Pallas kernels: 10.9 us -> 4.46 us  [the longest x1 2.15 us: shards(): pl.pallas_call(functools.partial(place_kernel, devices, slots), in_specs=...]
    unnamed x2 -> x6, local copies, waits for them, and re-layouts: 0.6 us -> 2.96 us
    all_to_all x1, blocking collectives: 21.6 us -> 19.7 us  [shards(): lax.all_to_all(outgoing, AXES, split_axis=0, concat_axis=0, tiled=True)]
    all_to_all x1, waiting for transfers between devices: 0.01 us -> 1.54 us  [shards(): lax.all_to_all(spread.reshape(devices, 1, LANES), AXES, split_axis=0, con...]
    convert_element_type x1 -> x0, other arithmetic: 0.7 us -> none  [shards(): keys = distinct_keys[0].reshape(slots, devices).T.astype(jnp.float32)]
    pad x1 -> x0, local copies, waits for them, and re-layouts: 0.69 us -> none  [shards(): keys = jnp.pad(keys, ((0, 0), (slots, LANES - 2 * slots)))]
  transfers between devices with their start and end apart: 1 -> 1, of which waited for: 0 -> 1; matrix products, arithmetic and copies ran while one was open for 4% -> 0% of each run, Pallas kernels for 12% -> 6%
where the time goes in v3:
time: 38 us; the launch traced here: 37.7 us
  blocking collectives  19.7 us (52%)
  starting transfers between devices  7.08 us (19%)
  Pallas kernels  5.06 us (13%)
  local copies, waits for them, and re-layouts  2.96 us (8%)
  waiting for transfers between devices  1.54 us (4%)
  between operations  1.32 us (3%)
    all_to_all x1, blocking collectives, shards(): lax.all_to_all(outgoing, AXES, split_axis=0, concat_axis=0, tiled=True)  19.7 us
    all_to_all x1, starting transfers between devices, shards(): lax.all_to_all(spread.reshape(devices, 1, LANES), AXES, split_axis=0, con...  7.08 us
    unnamed x6, local copies, waits for them, and re-layouts  2.96 us
    pallas_call x1, Pallas kernels, shards(): pl.pallas_call(functools.partial(place_kernel, devices, slots), in_specs=...  2.15 us
    pallas_call x1, Pallas kernels, shards(): pl.pallas_call(functools.partial(local_kernel, devices, slots, min(512, r...  2.11 us
    all_to_all x1, waiting for transfers between devices, shards(): lax.all_to_all(spread.reshape(devices, 1, LANES), AXES, split_axis=0, con...  1.54 us
  transfers between devices with their start and end apart: 1, of which 1 were waited for; matrix products, arithmetic and copies ran while one was open for 0% of the time, Pallas kernels for 6%

profile of v3, /device:TPU:1, one launch (start us, length us, event | category | flops | bytes accessed | tf_op | source)
XLA Modules:
  0.0 37.7 jit_solution(3343194986724754248)
XLA Ops:
  1.3 0.6 %spread.1 = s32[32,128]{1,0:T(8,128)} custom-call(s32[1]{0:T(128)S(6)} %copy.9.count_ref), custom_call_target="tpu_custom_call" | custom-call | tf_op jit(solution)/shard_map/spread/pallas_call | solution.py:145
  1.9 7.1 %all-to-all-start = ((s32[32,1,128]{2,1,0:T(1,128)}), s32[32,1,128]{2,1,0:T(1,128)S(1)}, u32[]{:S(2)}, u32[]{:S(2)}) async-start(s32[32,1,128]{2,1,0:T(1,128)} %bitcast.2), calls=%async_computation | async-start | bytes 32768 | tf_op jit(solution)/shard_map/all_to_all | solution.py:153
  9.0 0.0 copy-start
  9.0 1.6 %copy-done = f32[2048,256]{1,0:T(8,128)S(1)} copy-done((f32[2048,256]{1,0:T(8,128)S(1)}, f32[2048,256]{1,0:T(8,128)}, u32[]{:S(2)}) %copy-start) | copy-done | bytes 2097176
  10.6 0.0 copy-start.1
  10.6 0.7 %copy-done.1 = s32[2048]{0:T(1024)S(1)} copy-done((s32[2048]{0:T(1024)S(1)}, s32[2048]{0:T(1024)}, u32[]{:S(2)}) %copy-start.1) | copy-done | bytes 8216
  11.3 0.0 copy-start.2
  11.3 0.7 %copy-done.2 = s32[1,512]{1,0:T(1,128)S(1)} copy-done((s32[1,512]{1,0:T(1,128)S(1)}, s32[1,512]{1,0:T(1,128)}, u32[]{:S(2)}) %copy-start.2) | copy-done | bytes 2072
  11.9 2.1 %local.1 = f32[2112,128]{1,0:T(8,128)S(1)} custom-call(s32[1,2048]{1,0:T(1,128)S(1)} %bitcast.15, f32[2048,256]{1,0:T(8,128)S(1)} %copy-done, s32[1,512]{1,0:T(1,128)S(1)} %copy-done.2), custom_call_target="tpu_custom_call" | custom-call | flops 1610612736 | bytes 2097152 | tf_op jit(solution)/shard_map/local/pallas_call | solution.py:155
  14.1 1.5 %all-to-all-done = s32[32,1,128]{2,1,0:T(1,128)S(1)} async-done(((s32[32,1,128]{2,1,0:T(1,128)}), s32[32,1,128]{2,1,0:T(1,128)S(1)}, u32[]{:S(2)}, u32[]{:S(2)}) %all-to-all-start) | async-done | bytes 16416 | tf_op jit(solution)/shard_map/all_to_all | solution.py:153
  15.6 0.2 roll.1
  15.8 19.7 %all_to_all.10 = f32[32,1,4224]{2,1,0:T(1,128)S(1)} all-to-all(f32[32,1,4224]{2,1,0:T(1,128)S(1)} %roll.1), channel_id=1, replica_groups=mesh['gx'=4,'gy'=2,'gz'=4] {'gx','gy','gz'}, dimensions={0} | all-to-all | bytes 1081344 | tf_op jit(solution)/shard_map/all_to_all | solution.py:178
  35.5 2.1 %place.1 = (f32[512,256]{1,0:T(8,128)}, s32[4,128]{1,0:T(4,128)}, s32[4,128]{1,0:T(4,128)}, s32[1]{0:T(128)}) custom-call(s32[1]{0:T(128)} %bitcast.me_ref, s32[32,128]{1,0:T(8,128)S(1)} %bitcast.14, f32[1056,128]{1,0:T(8,128)S(1)} %bitcast.11), custom_call_target="tpu_custom_call" | custom-call | tf_op jit(solution)/shard_map/place/pallas_call | solution.py:179
Async XLA Ops:
  1.9 13.7 %all-to-all-start = ((s32[32,1,128]{2,1,0:T(1,128)}), s32[32,1,128]{2,1,0:T(1,128)S(1)}, u32[]{:S(2)}, u32[]{:S(2)}) async-start(s32[32,1,128]{2,1,0:T(1,128)} %bitcast.2), calls=%async_computation | async-start | bytes 32768 | tf_op jit(solution)/shard_map/all_to_all | solution.py:153
  9.0 1.6 %copy-start = (f32[2048,256]{1,0:T(8,128)S(1)}, f32[2048,256]{1,0:T(8,128)}, u32[]{:S(2)}) copy-start(f32[2048,256]{1,0:T(8,128)} %values_ref.1) | copy-start | bytes 6291460
  10.6 0.7 %copy-start.1 = (s32[2048]{0:T(1024)S(1)}, s32[2048]{0:T(1024)}, u32[]{:S(2)}) copy-start(s32[2048]{0:T(1024)} %param.5) | copy-start | bytes 24580
  11.3 0.7 %copy-start.2 = (s32[1,512]{1,0:T(1,128)S(1)}, s32[1,512]{1,0:T(1,128)}, u32[]{:S(2)}) copy-start(s32[1,512]{1,0:T(1,128)} %keys_ref.1) | copy-start | bytes 6148

commit v4 on v3

--- a/solution.py
+++ b/solution.py
@@ -20,7 +20,18 @@
     return high, middle, low
 
 
-def local_kernel(devices, slots, block, index_ref, values_ref, keys_ref, packed_ref, sums_ref, fields_ref):
+def local_kernel(
+    devices, slots, block, all_index_ref, all_values_ref, all_keys_ref, packed_ref,
+    index_ref, values_ref, keys_ref, sums_ref, fields_ref, index_sem, keys_sem, sem
+):
+    index_copy = pltpu.make_async_copy(all_index_ref, index_ref, index_sem)
+    keys_copy = pltpu.make_async_copy(all_keys_ref, keys_ref, keys_sem)
+    copies = [
+        pltpu.make_async_copy(all_values_ref.at[pl.ds(start, block)], values_ref.at[pl.ds(start, block)], sem.at[step])
+        for step, start in enumerate(range(0, values_ref.shape[0], block))
+    ]
+    for copy in [keys_copy, index_copy] + copies:
+        copy.start()
     span, width = sums_ref.shape
     rows = values_ref.shape[0]
     parts = width // LANES
@@ -33,16 +44,19 @@
         return lax.dot_general(left, right, (((1,), (1,)), ((), ())), preferred_element_type=jnp.float32)
 
     group = lax.broadcasted_iota(jnp.int32, (1, span), 1)
+    keys_copy.wait()
     to_residue = one_hot(devices, group % devices).astype(jnp.bfloat16)
     to_level = jnp.where(one_hot(LANES, group // devices + slots), keys_ref[...].astype(jnp.float32), 0.0)
     fields = jnp.zeros(fields_ref.shape, jnp.float32)
     for part in split3(to_level):
         fields = fields + across(to_residue, part)
-    for start in range(0, rows, block):
+    index_copy.wait()
+    for step, start in enumerate(range(0, rows, block)):
         index = index_ref[:, start : start + block]
         residue = index % devices
         level = index // devices
         hits = one_hot(span, residue * slots + level).astype(jnp.bfloat16)
+        copies[step].wait()
         high, middle, low = split3(values_ref[start : start + block, :])
         total = jnp.dot(hits, high, preferred_element_type=jnp.float32)
         total = total + jnp.dot(hits, middle, preferred_element_type=jnp.float32)
@@ -152,14 +166,24 @@
     )(group_counts)
     counts = lax.all_to_all(spread.reshape(devices, 1, LANES), AXES, split_axis=0, concat_axis=0, tiled=True)
     counts = counts.reshape(devices, LANES)
+    block = min(512, rows)
     packed = pl.pallas_call(
-        functools.partial(local_kernel, devices, slots, min(512, rows)),
-        in_specs=[pl.BlockSpec(memory_space=pltpu.VMEM)] * 3,
+        functools.partial(local_kernel, devices, slots, block),
+        in_specs=[pl.BlockSpec(memory_space=pl.ANY)] * 3,
         out_specs=pl.BlockSpec(memory_space=pltpu.VMEM),
         out_shape=jax.ShapeDtypeStruct((2 * devices * each, LANES), jnp.float32),
-        scratch_shapes=[pltpu.VMEM((span, width), jnp.float32), pltpu.VMEM((devices, LANES), jnp.float32)],
+        scratch_shapes=[
+            pltpu.VMEM((1, rows), jnp.int32),
+            pltpu.VMEM((rows, width), jnp.float32),
+            pltpu.VMEM((1, span), jnp.int32),
+            pltpu.VMEM((span, width), jnp.float32),
+            pltpu.VMEM((devices, LANES), jnp.float32),
+            pltpu.SemaphoreType.DMA,
+            pltpu.SemaphoreType.DMA,
+            pltpu.SemaphoreType.DMA((rows // block,)),
+        ],
         cost_estimate=pl.CostEstimate(flops=6 * span * rows * width, bytes_accessed=4 * rows * width, transcendentals=0),
-        compiler_params=pltpu.CompilerParams(vmem_limit_bytes=16 * MIB),
+        compiler_params=pltpu.CompilerParams(vmem_limit_bytes=52 * MIB),
         name="local",
     )(group_index.reshape(1, rows), measures, distinct_keys)
     outgoing = pl.pallas_call(
@@ -169,7 +193,7 @@
             pl.BlockSpec(memory_space=pltpu.VMEM),
             pl.BlockSpec(memory_space=pltpu.VMEM),
         ],
-        out_specs=pl.BlockSpec(memory_space=pltpu.HBM),
+        out_specs=pl.BlockSpec(memory_space=pl.ANY),
         out_shape=jax.ShapeDtypeStruct((devices, 1, each * LANES), jnp.float32),
         scratch_shapes=[pltpu.SemaphoreType.DMA],
         compiler_params=pltpu.CompilerParams(vmem_limit_bytes=4 * MIB),

time: 38 us -> 39.3 us (1.034)
  Pallas kernels: 5.06 us -> 7.97 us
  local copies, waits for them, and re-layouts: 2.96 us -> 1.37 us
  waiting for transfers between devices: 1.54 us -> 0.23 us
  blocking collectives: 19.7 us -> 21 us
    pallas_call x1, Pallas kernels: 2.11 us -> 5.01 us  [shards(): pl.pallas_call(functools.partial(local_kernel, devices, slots, block), in...]
    unnamed x6 -> x4, local copies, waits for them, and re-layouts: 2.96 us -> 1.37 us
    all_to_all x1, waiting for transfers between devices: 1.54 us -> 0.23 us  [shards(): lax.all_to_all(spread.reshape(devices, 1, LANES), AXES, split_axis=0, con...]
    all_to_all x1, blocking collectives: 19.7 us -> 21 us  [shards(): lax.all_to_all(outgoing, AXES, split_axis=0, concat_axis=0, tiled=True)]
  transfers between devices with their start and end apart: 1 -> 1, of which waited for: 1 -> 1; matrix products, arithmetic and copies ran while one was open for 0% -> 0% of each run, Pallas kernels for 6% -> 13%
where the time goes in v4:
time: 39.3 us; the launch traced here: 39 us
  blocking collectives  21 us (53%)
  Pallas kernels  7.97 us (20%)
  starting transfers between devices  7.08 us (18%)
  local copies, waits for them, and re-layouts  1.37 us (3%)
  between operations  1.32 us (3%)
    all_to_all x1, blocking collectives, shards(): lax.all_to_all(outgoing, AXES, split_axis=0, concat_axis=0, tiled=True)  21 us
    all_to_all x1, starting transfers between devices, shards(): lax.all_to_all(spread.reshape(devices, 1, LANES), AXES, split_axis=0, con...  7.08 us
    pallas_call x1, Pallas kernels, shards(): pl.pallas_call(functools.partial(local_kernel, devices, slots, block), in...  5.01 us
    pallas_call x1, Pallas kernels, shards(): pl.pallas_call(functools.partial(place_kernel, devices, slots), in_specs=...  2.16 us
    unnamed x4, local copies, waits for them, and re-layouts  1.37 us
  transfers between devices with their start and end apart: 1, of which 1 were waited for; matrix products, arithmetic and copies ran while one was open for 0% of the time, Pallas kernels for 13%

profile of v4, /device:TPU:1, one launch (start us, length us, event | category | flops | bytes accessed | tf_op | source)
XLA Modules:
  0.0 39.0 jit_solution(3137683690531525320)
XLA Ops:
  1.3 0.6 %spread.1 = s32[32,128]{1,0:T(8,128)} custom-call(s32[1]{0:T(128)S(6)} %copy.9.count_ref), custom_call_target="tpu_custom_call" | custom-call | tf_op jit(solution)/shard_map/spread/pallas_call | solution.py:159
  1.9 7.1 %all-to-all-start = ((s32[32,1,128]{2,1,0:T(1,128)}), s32[32,1,128]{2,1,0:T(1,128)S(1)}, u32[]{:S(2)}, u32[]{:S(2)}) async-start(s32[32,1,128]{2,1,0:T(1,128)} %bitcast.2), calls=%async_computation | async-start | bytes 32768 | tf_op jit(solution)/shard_map/all_to_all | solution.py:167
  9.0 0.0 copy-start
  9.0 0.7 %copy-done = s32[2048]{0:T(1024)S(1)} copy-done((s32[2048]{0:T(1024)S(1)}, s32[2048]{0:T(1024)}, u32[]{:S(2)}) %copy-start) | copy-done | bytes 8216
  9.7 0.0 copy-start.1
  9.7 0.7 %copy-done.1 = s32[1,512]{1,0:T(1,128)S(1)} copy-done((s32[1,512]{1,0:T(1,128)S(1)}, s32[1,512]{1,0:T(1,128)}, u32[]{:S(2)}) %copy-start.1) | copy-done | bytes 2072
  10.4 5.0 %local.1 = f32[2112,128]{1,0:T(8,128)S(1)} custom-call(s32[1,2048]{1,0:T(1,128)S(1)} %bitcast.15, f32[2048,256]{1,0:T(8,128)} %all_values_ref.1, s32[1,512]{1,0:T(1,128)S(1)} %copy-done.1), custom_call_target="tpu_custom_call" | custom-call | flops 1610612736 | bytes 2097152 | tf_op jit(solution)/shard_map/local/pallas_call | solution.py:170
  15.4 0.2 all-to-all-done
  15.6 0.2 roll.1
  15.8 21.0 %all_to_all.10 = f32[32,1,4224]{2,1,0:T(1,128)S(1)} all-to-all(f32[32,1,4224]{2,1,0:T(1,128)S(1)} %roll.1), channel_id=1, replica_groups=mesh['gx'=4,'gy'=2,'gz'=4] {'gx','gy','gz'}, dimensions={0} | all-to-all | bytes 1081344 | tf_op jit(solution)/shard_map/all_to_all | solution.py:202
  36.9 2.2 %place.1 = (f32[512,256]{1,0:T(8,128)}, s32[4,128]{1,0:T(4,128)}, s32[4,128]{1,0:T(4,128)}, s32[1]{0:T(128)}) custom-call(s32[1]{0:T(128)} %bitcast.me_ref, s32[32,128]{1,0:T(8,128)S(1)} %bitcast.14, f32[1056,128]{1,0:T(8,128)S(1)} %bitcast.11), custom_call_target="tpu_custom_call" | custom-call | tf_op jit(solution)/shard_map/place/pallas_call | solution.py:203
Async XLA Ops:
  1.9 13.7 %all-to-all-start = ((s32[32,1,128]{2,1,0:T(1,128)}), s32[32,1,128]{2,1,0:T(1,128)S(1)}, u32[]{:S(2)}, u32[]{:S(2)}) async-start(s32[32,1,128]{2,1,0:T(1,128)} %bitcast.2), calls=%async_computation | async-start | bytes 32768 | tf_op jit(solution)/shard_map/all_to_all | solution.py:167
  9.0 0.7 %copy-start = (s32[2048]{0:T(1024)S(1)}, s32[2048]{0:T(1024)}, u32[]{:S(2)}) copy-start(s32[2048]{0:T(1024)} %param.5) | copy-start | bytes 24580
  9.7 0.7 %copy-start.1 = (s32[1,512]{1,0:T(1,128)S(1)}, s32[1,512]{1,0:T(1,128)}, u32[]{:S(2)}) copy-start(s32[1,512]{1,0:T(1,128)} %all_keys_ref.1) | copy-start | bytes 6148
